TPU v7x, 32 devices: a whole 2x2x4 slice. The times are simulated.
32 devices in a mesh: batch: 2 (over y), space: 8 (over z, x), hidden: 2 (over core).
Axes of the slice: x: 2, y: 2, z: 4, core: 2. Of those that a mesh axis runs over, the one named last changes fastest.
Arguments:
- nodes: bfloat16 [2, 1024, 512], P('batch', 'space'), may hold values from -6 to 6
- edges: bfloat16 [2, 8192, 512], P('batch', 'space'), may hold values from -6 to 6
- node_cotangent: bfloat16 [2, 1024, 512], P('batch', 'space'), may hold values from -18 to 18
- edge_cotangent: bfloat16 [2, 8192, 512], P('batch', 'space'), may hold values from -18 to 18
- senders: int32 [8192], P('space'), may hold values from 0 to 255
- receivers: int32 [8192], P('space'), may hold values from 0 to 127
- send_lists: int32 [8, 2, 64], P('space'), may hold values from 0 to 127
- edge_first: bfloat16 [1536, 512], P(None, 'hidden'), may hold values from -0.15625 to 0.15625
- edge_bias: float32 [512], P('hidden'), may hold values from -3 to 3
- edge_second: bfloat16 [512, 512], P('hidden'), may hold values from -0.25 to 0.25
- edge_gain: float32 [512], replicated, may hold values from 0.1 to 1.9
- node_first: bfloat16 [1024, 512], replicated, may hold values from -0.1875 to 0.1875
- node_bias: float32 [512], replicated, may hold values from -3 to 3
- node_second: bfloat16 [512, 512], replicated, may hold values from -0.25 to 0.25
- node_gain: float32 [512], replicated, may hold values from 0.1 to 1.9
Outputs:
- grad_nodes: bfloat16 [2, 1024, 512], P('batch', 'space', 'hidden')
- grad_edges: bfloat16 [2, 8192, 512], P('batch', 'space', 'hidden')
- grad_edge_first: float32 [1536, 512], P(None, 'hidden')
- grad_edge_bias: float32 [512], P('hidden')
- grad_edge_second: float32 [512, 512], P('hidden')
- grad_edge_gain: float32 [512], replicated
- grad_node_first: float32 [1024, 512], replicated
- grad_node_bias: float32 [512], replicated
- grad_node_second: float32 [512, 512], replicated
- grad_node_gain: float32 [512], replicated
Inputs may be any that keep to these rules, and one draw needn't show every extreme that they name: `senders`: an entry below 128 is a local node of the edge's patch; 128 + k is row k of the previous patch's list 1, 192 + k row k of the next patch's list 0. `receivers`: local nodes of the edge's patch. `send_lists`: local nodes of the patch; entries may repeat.
All inputs are finite; a program needn't handle non-finite values.
Results may differ from a plain program's by a relative error of at most 0.015.
Values may be sent and summed in bfloat16 or wider, within the bound.
A program may use at most 128 MiB of HBM per device.

v0:
```python
import jax
import jax.numpy as jnp
from jax import lax
from jax.sharding import PartitionSpec as P

EPS = 1e-05


def extended(cells, sides, width):
    for axis, dim in sides:
        count = lax.axis_size(axis)
        head = lax.slice_in_dim(cells, 0, width, axis=dim)
        tail = lax.slice_in_dim(cells, cells.shape[dim] - width, cells.shape[dim], axis=dim)
        cells = jnp.concatenate(
            [
                lax.ppermute(tail, axis, [(i, (i + 1) % count) for i in range(count)]),
                cells,
                lax.ppermute(head, axis, [((i + 1) % count, i) for i in range(count)]),
            ],
            axis=dim,
        )
    return cells


def one_hot(indices, columns, wanted):
    return (indices[:, None] == jnp.arange(columns, dtype=jnp.int32)[None, :]).astype(wanted)


def matmul(lefthand, righthand):
    return jnp.dot(lefthand, righthand, preferred_element_type=jnp.float32)


def matmul_tn(lefthand, righthand):
    return lax.dot_general(
        lefthand, righthand, (((0,), (0,)), ((), ())), preferred_element_type=jnp.float32
    )


def matmul_nt(lefthand, righthand):
    return lax.dot_general(
        lefthand, righthand, (((1,), (1,)), ((), ())), preferred_element_type=jnp.float32
    )


def exact_tn(lefthand, righthand):
    return lax.dot_general(
        lefthand,
        righthand,
        (((0,), (0,)), ((), ())),
        precision=lax.Precision.HIGHEST,
        preferred_element_type=jnp.float32,
    )


def normalize(values):
    centre = values - jnp.mean(values, axis=-1, keepdims=True)
    scaled = lax.rsqrt(jnp.mean(centre * centre, axis=-1, keepdims=True) + EPS)
    return (centre * scaled, scaled)


def norm_back(upstream, gain_vec, normed, scaled):
    pulled = upstream * gain_vec
    return scaled * (
        pulled
        - jnp.mean(pulled, axis=-1, keepdims=True)
        - normed * jnp.mean(pulled * normed, axis=-1, keepdims=True)
    )


def silu_slope(values):
    logistic = jax.nn.sigmoid(values)
    return logistic * (1.0 + values * (1.0 - logistic))


def on_device(
    nodes,
    edges,
    node_cotangent,
    edge_cotangent,
    senders,
    receivers,
    send_lists,
    edge_first,
    edge_bias,
    edge_second,
    edge_gain,
    node_first,
    node_bias,
    node_second,
    node_gain,
):
    splits = lax.axis_size("hidden")
    my_part = lax.axis_index("hidden")
    width = nodes.shape[2]
    half = width // splits
    node_rows = nodes[0]
    node_count = node_rows.shape[0]
    halo_count = send_lists.shape[2]
    listed = send_lists[0].reshape(-1)
    picker = one_hot(listed, node_count, jnp.bfloat16)
    outgoing = matmul(picker, node_rows).astype(jnp.bfloat16).reshape(2, halo_count, width)
    padded = extended(outgoing, (("space", 0),), 1)
    table = jnp.concatenate([node_rows, padded[0], padded[3]], axis=0)
    table_rows = table.shape[0]
    sender_hot = one_hot(senders, table_rows, jnp.bfloat16)
    receiver_hot = one_hot(receivers, node_count, jnp.bfloat16)
    from_sender = matmul(sender_hot, table).astype(jnp.bfloat16)
    from_receiver = matmul(receiver_hot, node_rows).astype(jnp.bfloat16)
    edge_input = jnp.concatenate([edges[0], from_sender, from_receiver], axis=1)
    edge_pre = matmul(edge_input, edge_first) + edge_bias
    edge_act = jax.nn.silu(edge_pre).astype(jnp.bfloat16)
    edge_total = lax.psum(matmul(edge_act, edge_second).astype(jnp.bfloat16), "hidden").astype(
        jnp.float32
    )
    edge_normed, edge_scale = normalize(edge_total)
    message = (edge_gain * edge_normed).astype(jnp.bfloat16)
    gathered = matmul_tn(receiver_hot, message).astype(jnp.bfloat16)
    node_input = jnp.concatenate([node_rows, gathered], axis=1)
    node_pre = matmul(node_input, node_first) + node_bias
    node_act = jax.nn.silu(node_pre).astype(jnp.bfloat16)
    node_normed, node_scale = normalize(matmul(node_act, node_second))
    node_upstream = node_cotangent[0].astype(jnp.float32)
    node_gain_grad = jnp.sum(node_upstream * node_normed, axis=0)
    node_dz = norm_back(node_upstream, node_gain, node_normed, node_scale).astype(jnp.bfloat16)
    node_second_grad = matmul_tn(node_act, node_dz)
    node_dh = (matmul_nt(node_dz, node_second) * silu_slope(node_pre)).astype(jnp.bfloat16)
    node_first_grad = matmul_tn(node_input, node_dh)
    node_bias_grad = jnp.sum(node_dh.astype(jnp.float32), axis=0)
    node_dx = matmul_nt(node_dh, node_first)
    agg_grad = node_dx[:, width:].astype(jnp.bfloat16)
    edge_upstream = edge_cotangent[0].astype(jnp.float32)
    message_grad = edge_upstream + matmul(receiver_hot, agg_grad)
    edge_gain_grad = jnp.sum(message_grad * edge_normed, axis=0)
    edge_dz = norm_back(message_grad, edge_gain, edge_normed, edge_scale).astype(jnp.bfloat16)
    edge_second_grad = matmul_tn(edge_act, edge_dz)
    edge_dh = (matmul_nt(edge_dz, edge_second) * silu_slope(edge_pre)).astype(jnp.bfloat16)
    edge_first_grad = matmul_tn(edge_input, edge_dh)
    edge_bias_grad = jnp.sum(edge_dh.astype(jnp.float32), axis=0)
    sender_exact = one_hot(senders, table_rows, jnp.float32)
    receiver_exact = one_hot(receivers, node_count, jnp.float32)
    blocks = edge_first.reshape(3, splits, half, edge_first.shape[1])
    mine = lax.all_to_all(blocks, "hidden", split_axis=1, concat_axis=3, tiled=True).reshape(
        3 * half, -1
    )
    input_grad = matmul_nt(lax.all_gather(edge_dh, "hidden", axis=1, tiled=True), mine)
    edge_own = input_grad[:, :half]
    sender_grad = exact_tn(sender_exact, input_grad[:, half : 2 * half])
    receiver_grad = exact_tn(receiver_exact, input_grad[:, 2 * half :])
    table_grad = jnp.concatenate(
        [sender_grad[:node_count] + receiver_grad, sender_grad[node_count:]], axis=0
    )
    returning = jnp.stack(
        [table_grad[node_count : node_count + halo_count], table_grad[node_count + halo_count :]],
        axis=0,
    )
    returned = extended(returning.astype(jnp.bfloat16), (("space", 0),), 1).astype(returning.dtype)
    arriving = jnp.concatenate([returned[0], returned[3]], axis=0)
    halo_grad = exact_tn(one_hot(listed, node_count, jnp.float32), arriving)
    own_cot = lax.dynamic_slice_in_dim(node_upstream, my_part * half, half, 1)
    own_node = lax.dynamic_slice_in_dim(node_dx, my_part * half, half, 1)
    grad_nodes = (own_cot + own_node + table_grad[:node_count] + halo_grad).astype(jnp.bfloat16)[
        None
    ]
    own_edge_cot = lax.dynamic_slice_in_dim(edge_upstream, my_part * half, half, 1)
    grad_edges = (own_edge_cot + edge_own).astype(jnp.bfloat16)[None]
    (
        edge_first_grad,
        edge_bias_grad,
        edge_second_grad,
        edge_gain_grad,
        node_first_grad,
        node_bias_grad,
        node_second_grad,
        node_gain_grad,
    ) = lax.psum(
        (
            edge_first_grad,
            edge_bias_grad,
            edge_second_grad,
            edge_gain_grad,
            node_first_grad,
            node_bias_grad,
            node_second_grad,
            node_gain_grad,
        ),
        ("batch", "space"),
    )
    return (
        grad_nodes,
        grad_edges,
        edge_first_grad,
        edge_bias_grad,
        edge_second_grad,
        edge_gain_grad,
        node_first_grad,
        node_bias_grad,
        node_second_grad,
        node_gain_grad,
    )


def solution(mesh):
    placed = (
        P("batch", "space", None),
        P("batch", "space", None),
        P("batch", "space", None),
        P("batch", "space", None),
        P("space"),
        P("space"),
        P("space", None, None),
        P(None, "hidden"),
        P("hidden"),
        P("hidden", None),
        P(),
        P(),
        P(),
        P(),
        P(),
    )
    return jax.shard_map(
        on_device,
        mesh=mesh,
        in_specs=placed,
        out_specs=(
            P("batch", "space", "hidden"),
            P("batch", "space", "hidden"),
            P(None, "hidden"),
            P("hidden"),
            P("hidden", None),
            P(),
            P(),
            P(),
            P(),
            P(),
        ),
        check_vma=False,
    )
```

profile of v0, /device:TPU:0, one launch (start us, length us, event | category | flops | bytes accessed | tf_op | source)
XLA Modules:
  0.0 280.4 jit_solution(7566066074686124205)
XLA Ops:
  8.7 1.1 convolution_convert_fusion.4
  9.8 3.0 %collective-permute-start = (bf16[1,64,512]{2,1,0:T(8,128)(2,1)S(1)}, bf16[1,64,512]{2,1,0:T(8,128)(2,1)S(1)}, u32[]{:S(2)}, u32[]{:S(2)}) collective-permute-start(bf16[1,64,512]{2,1,0:T(8,128)(2,1)S(1)} %get-tuple-element.28), channel_id=1, source_target_pairs={{0,2},{2,4},{4,6},{6,8},{8,10},{10,12},{12,14},{14,0},{1,3},{3,5},... | collective-permute-start | bytes 196616 | tf_op jit(solution)/shard_map/ppermute | solution.py:16
  12.9 3.1 %collective-permute-start.1 = (bf16[1,64,512]{2,1,0:T(8,128)(2,1)S(1)}, bf16[1,64,512]{2,1,0:T(8,128)(2,1)S(1)}, u32[]{:S(2)}, u32[]{:S(2)}) collective-permute-start(bf16[1,64,512]{2,1,0:T(8,128)(2,1)S(1)} %get-tuple-element.29), channel_id=1, source_target_pairs={{2,0},{4,2},{6,4},{8,6},{10,8},{12,10},{14,12},{0,14},{3,1},{5,3},... | collective-permute-start | bytes 196616 | tf_op jit(solution)/shard_map/ppermute | solution.py:18
  16.0 1.5 convolution_convert_fusion.2
  17.5 1.3 copy.33
  19.4 2.9 %convolution_add_fusion = f32[1024,256]{1,0:T(8,128)S(1)} fusion(bf16[1536,256]{1,0:T(8,128)(2,1)} %param.22, bf16[1024,512]{0,1:T(8,128)(2,1)S(1)} %convolution_convert_fusion.2, bf16[1024,512]{0,1:T(8,128)(2,1)S(1)} %convolution_convert_fusion, bf16[1024,512]{0,1:T(8,128)(2,1)} %bitcast.76, f32[256]{0:T(256)S(1)} %copy-done.35), kind=kOutput, calls=%fused_computation.22 | convolution fusion | flops 815005696 | bytes 4981760 | tf_op jit(solution)/shard_map/dot_general | solution.py:30
  22.3 1.4 convolution_convert_fusion.1
  23.8 20.5 %all-reduce.5.cloned.1.call-done = bf16[1024,512]{1,0:T(8,128)(2,1)} async-done(((bf16[1024,512]{1,0:T(8,128)(2,1)}), bf16[1024,512]{1,0:T(8,128)(2,1)}) %all-reduce.5.cloned.1.call-update) | async-done | bytes 1048592 | tf_op jit(solution)/shard_map/psum | solution.py:112
  44.4 1.5 convert_reduce_fusion
  45.9 1.7 fusion.12
  51.9 1.9 fusion.11
  55.1 1.9 convert_reduce_fusion.1
  57.1 2.5 fusion.55
  59.6 2.7 fusion.41
  62.4 1.3 fusion.57
  64.3 2.1 fusion.14
  66.4 1.1 copy-done.9
  68.5 4.4 %all-to-all-start = ((bf16[3,2,256,256]{3,2,0,1:T(8,128)(2,1)}), bf16[3,2,256,256]{3,2,0,1:T(8,128)(2,1)}, u32[]{:S(2)}, u32[]{:S(2)}) async-start(bf16[3,2,256,256]{3,2,0,1:T(8,128)(2,1)} %copy.35), calls=%async_computation | async-start | bytes 1572864 | tf_op jit(solution)/shard_map/all_to_all | solution.py:142
  72.9 1.5 convert_element_type.87
  75.0 1.9 copy.36
  76.9 1.1 copy.38
  78.0 46.1 %all-reduce = (f32[256]{0:T(256)}, f32[512]{0:T(512)}, f32[512]{0:T(512)}, f32[512]{0:T(512)}) all-reduce(f32[256]{0:T(256)S(1)} %copy-done.28, f32[512]{0:T(512)S(1)} %copy-done.27, f32[512]{0:T(512)S(1)} %copy-done.26, f32[512]{0:T(512)S(1)} %get-tuple-element.13), channel_id=1, replica_groups=mesh['batch'=2,'space'=8,'hidden'=2] {'batch','space'}, use_global_device_ids=true, to_apply=%region_11.12 | all-reduce | flops 1792 | bytes 14336 | tf_op jit(solution)/shard_map/psum | solution.py:175
  124.1 2.5 fusion.61
  126.6 1.2 fusion.59
  127.9 4.7 %collective-permute-start.3 = (bf16[1,64,256]{2,1,0:T(8,128)(2,1)S(1)}, bf16[1,64,256]{2,1,0:T(8,128)(2,1)S(1)}, u32[]{:S(2)}, u32[]{:S(2)}) collective-permute-start(bf16[1,64,256]{2,1,0:T(8,128)(2,1)S(1)} %get-tuple-element.27), channel_id=1, source_target_pairs={{2,0},{4,2},{6,4},{8,6},{10,8},{12,10},{14,12},{0,14},{3,1},{5,3},... | collective-permute-start | bytes 98312 | tf_op jit(solution)/shard_map/ppermute | solution.py:18
  132.6 1.0 fusion.27
  133.5 1.7 fusion.16
  135.3 1.0 fusion.18
  136.3 131.0 %all-reduce.7.cloned.1.call-done = (f32[1536,256]{1,0:T(8,128)}, f32[256,512]{1,0:T(8,128)}, f32[1024,512]{1,0:T(8,128)}, f32[512,512]{1,0:T(8,128)}) async-done(((f32[1536,256]{1,0:T(8,128)}, f32[256,512]{1,0:T(8,128)}, f32[1024,512]{1,0:T(8,128)}, f32[512,512]{1,0:T(8,128)}), (f32[1536,256]{1,0:T(8,128)}, f32[256,512]{1,0:T(8,128)}, f32[1024,512]{1,0:T(8,128)}, ...) | async-done | bytes 5242896 | tf_op jit(solution)/shard_map/psum | solution.py:175
  267.3 2.8 copy.44
  270.9 1.3 copy.46
  272.9 1.0 copy.47
  (117 shorter events, 11.2 us)
Async XLA Ops:
  7.2 41.4 %copy-start = (bf16[1024,512]{1,0:T(8,128)(2,1)S(1)}, bf16[1024,512]{1,0:T(8,128)(2,1)}, u32[]{:S(2)}) copy-start(bf16[1024,512]{1,0:T(8,128)(2,1)} %param.26) | copy-start | bytes 3145732
  7.2 11.6 %copy-start.2 = (bf16[1,128,512]{2,1,0:T(8,128)(2,1)S(1)}, bf16[1,128,512]{2,1,0:T(8,128)(2,1)}, u32[]{:S(2)}) copy-start(bf16[1,128,512]{2,1,0:T(8,128)(2,1)} %param.15) | copy-start | bytes 393220
  7.2 10.2 %copy-start.5 = (bf16[1,1024,512]{2,1,0:T(8,128)(2,1)S(1)}, bf16[1,1024,512]{2,1,0:T(8,128)(2,1)}, u32[]{:S(2)}) copy-start(bf16[1,1024,512]{2,1,0:T(8,128)(2,1)} %param.16) | copy-start | bytes 3145732
  7.2 11.6 %copy-start.18 = (s32[1024]{0:T(1024)S(1)}, s32[1024]{0:T(1024)}, u32[]{:S(2)}) copy-start(s32[1024]{0:T(1024)} %param.19) | copy-start | bytes 12292
  7.2 37.1 %all-reduce.5.cloned.1.call-start = ((), (), s32[]{:S(2)}) async-start(), calls=%async_computation.1 | async-start | bytes 2097152 | tf_op jit(solution)/shard_map/psum | solution.py:112
  9.8 8.9 %collective-permute-start = (bf16[1,64,512]{2,1,0:T(8,128)(2,1)S(1)}, bf16[1,64,512]{2,1,0:T(8,128)(2,1)S(1)}, u32[]{:S(2)}, u32[]{:S(2)}) collective-permute-start(bf16[1,64,512]{2,1,0:T(8,128)(2,1)S(1)} %get-tuple-element.28), channel_id=1, source_target_pairs={{0,2},{2,4},{4,6},{6,8},{8,10},{10,12},{12,14},{14,0},{1,3},{3,5},... | collective-permute-start | bytes 196616 | tf_op jit(solution)/shard_map/ppermute | solution.py:16
  12.9 5.9 %collective-permute-start.1 = (bf16[1,64,512]{2,1,0:T(8,128)(2,1)S(1)}, bf16[1,64,512]{2,1,0:T(8,128)(2,1)S(1)}, u32[]{:S(2)}, u32[]{:S(2)}) collective-permute-start(bf16[1,64,512]{2,1,0:T(8,128)(2,1)S(1)} %get-tuple-element.29), channel_id=1, source_target_pairs={{2,0},{4,2},{6,4},{8,6},{10,8},{12,10},{14,12},{0,14},{3,1},{5,3},... | collective-permute-start | bytes 196616 | tf_op jit(solution)/shard_map/ppermute | solution.py:18
  19.4 2.9 %copy-start.36 = (bf16[1024,512]{0,1:T(8,128)(2,1)}, bf16[1024,512]{0,1:T(8,128)(2,1)S(1)}, u32[]{:S(2)}) copy-start(bf16[1024,512]{0,1:T(8,128)(2,1)S(1)} %convolution_convert_fusion) | copy-start | bytes 3145732
  19.4 2.9 %copy-start.33 = (bf16[256,512]{1,0:T(8,128)(2,1)S(1)}, bf16[256,512]{1,0:T(8,128)(2,1)}, u32[]{:S(2)}) copy-start(bf16[256,512]{1,0:T(8,128)(2,1)} %param.24) | copy-start | bytes 786436
  23.8 23.8 %copy-start.17 = (s32[1024]{0:T(1024)S(1)}, s32[1024]{0:T(1024)}, u32[]{:S(2)}) copy-start(s32[1024]{0:T(1024)} %param.20) | copy-start | bytes 12292
  23.8 23.8 %copy-start.20 = (f32[512]{0:T(512)S(1)}, f32[512]{0:T(512)}, u32[]{:S(2)}) copy-start(f32[512]{0:T(512)} %param.25) | copy-start | bytes 6148
  23.8 100.3 %all-gather.2.cloned.1.call-start = ((), (), s32[]{:S(2)}) async-start(), calls=%async_computation.2 | async-start | bytes 1572864 | tf_op jit(solution)/shard_map/all_gather | solution.py:145
  44.3 3.3 %copy-start.1 = (bf16[1024,512]{1,0:T(8,128)(2,1)S(1)}, bf16[1024,512]{1,0:T(8,128)(2,1)}, u32[]{:S(2)}) copy-start(bf16[1024,512]{1,0:T(8,128)(2,1)} %all-reduce.5.cloned.1.call-done) | copy-start | bytes 3145732
  45.9 2.7 copy-start.19
  48.5 2.2 copy-start.12
  49.5 2.3 copy-start.29
  49.8 2.1 copy-start.4
  49.8 4.0 %copy-start.30 = (f32[128]{0:T(128)}, f32[128]{0:T(128)S(1)}, u32[]{:S(2)}) copy-start(f32[128]{0:T(128)S(1)} %get-tuple-element.39) | copy-start | bytes 1540
  49.8 3.9 %copy-start.31 = (f32[128]{0:T(128)}, f32[128]{0:T(128)S(1)}, u32[]{:S(2)}) copy-start(f32[128]{0:T(128)S(1)} %get-tuple-element.40) | copy-start | bytes 1540
  55.1 2.0 copy-start.22
  57.0 210.2 %all-reduce.7.cloned.1.call-start = ((), (), s32[]{:S(2)}) async-start(), calls=%async_computation.3 | async-start | bytes 10485760 | tf_op jit(solution)/shard_map/psum | solution.py:175
  57.1 5.3 %copy-start.40 = (f32[1024,256]{1,0:T(8,128)S(1)}, f32[1024,256]{1,0:T(8,128)}, u32[]{:S(2)}) copy-start(f32[1024,256]{1,0:T(8,128)} %copy-done.38) | copy-start | bytes 3145732
  68.5 6.0 %copy-start.11 = (bf16[1,128,512]{2,1,0:T(8,128)(2,1)S(1)}, bf16[1,128,512]{2,1,0:T(8,128)(2,1)}, u32[]{:S(2)}) copy-start(bf16[1,128,512]{2,1,0:T(8,128)(2,1)} %param.17) | copy-start | bytes 393220
  68.5 6.5 %all-to-all-start = ((bf16[3,2,256,256]{3,2,0,1:T(8,128)(2,1)}), bf16[3,2,256,256]{3,2,0,1:T(8,128)(2,1)}, u32[]{:S(2)}, u32[]{:S(2)}) async-start(bf16[3,2,256,256]{3,2,0,1:T(8,128)(2,1)} %copy.35), calls=%async_computation | async-start | bytes 1572864 | tf_op jit(solution)/shard_map/all_to_all | solution.py:142
  74.5 3.5 %copy-start.26 = (f32[512]{0:T(512)S(1)}, f32[512]{0:T(512)}, u32[]{:S(2)}) copy-start(f32[512]{0:T(512)} %get-tuple-element.37) | copy-start | bytes 6148
  74.5 3.5 %copy-start.27 = (f32[512]{0:T(512)S(1)}, f32[512]{0:T(512)}, u32[]{:S(2)}) copy-start(f32[512]{0:T(512)} %get-tuple-element.10) | copy-start | bytes 6148
  74.5 3.5 %copy-start.28 = (f32[256]{0:T(256)S(1)}, f32[256]{0:T(256)}, u32[]{:S(2)}) copy-start(f32[256]{0:T(256)} %get-tuple-element.35) | copy-start | bytes 3076
  127.8 7.5 %collective-permute-start.2 = (bf16[1,64,256]{2,1,0:T(8,128)(2,1)S(1)}, bf16[1,64,256]{2,1,0:T(8,128)(2,1)S(1)}, u32[]{:S(2)}, u32[]{:S(2)}) collective-permute-start(bf16[1,64,256]{2,1,0:T(8,128)(2,1)S(1)} %get-tuple-element.26), channel_id=1, source_target_pairs={{0,2},{2,4},{4,6},{6,8},{8,10},{10,12},{12,14},{14,0},{1,3},{3,5},... | collective-permute-start | bytes 98312 | tf_op jit(solution)/shard_map/ppermute | solution.py:16
  127.9 7.4 %copy-start.24 = (s32[128]{0:T(128)S(1)}, s32[128]{0:T(128)}, u32[]{:S(2)}) copy-start(s32[128]{0:T(128)} %copy-done.23) | copy-start | bytes 1540
  127.9 7.4 %collective-permute-start.3 = (bf16[1,64,256]{2,1,0:T(8,128)(2,1)S(1)}, bf16[1,64,256]{2,1,0:T(8,128)(2,1)S(1)}, u32[]{:S(2)}, u32[]{:S(2)}) collective-permute-start(bf16[1,64,256]{2,1,0:T(8,128)(2,1)S(1)} %get-tuple-element.27), channel_id=1, source_target_pairs={{2,0},{4,2},{6,4},{8,6},{10,8},{12,10},{14,12},{0,14},{3,1},{5,3},... | collective-permute-start | bytes 98312 | tf_op jit(solution)/shard_map/ppermute | solution.py:18
  267.3 2.8 %copy-start.13 = (f32[256,512]{1,0:T(8,128)S(1)}, f32[256,512]{1,0:T(8,128)}, u32[]{:S(2)}) copy-start(f32[256,512]{1,0:T(8,128)} %get-tuple-element.45) | copy-start | bytes 1572868
  267.3 3.6 %copy-start.3 = (f32[1024,512]{1,0:T(8,128)S(1)}, f32[1024,512]{1,0:T(8,128)}, u32[]{:S(2)}) copy-start(f32[1024,512]{1,0:T(8,128)} %get-tuple-element.47) | copy-start | bytes 6291460
  (17 other events, 22.9 us)
Sparse Core Ops, SparseCore 0:
  23.9 20.3 all-reduce.4
  57.2 9.9 all-gather.1
  73.9 193.3 all-reduce.6
where the time goes:
time: 281 us; the launch traced here: 280 us
  waiting for transfers between devices  152 us (54%)
  blocking collectives  46.1 us (16%)
  matrix products  29.2 us (10%)
  local copies, waits for them, and re-layouts  16.2 us (6%)
  starting transfers between devices  15.4 us (5%)
  between operations  14.3 us (5%)
  other arithmetic  7.05 us (3%)
    psum x1, waiting for transfers between devices, on_device(): lax.psum((edge_first_grad, edge_bias_grad, edge_second_grad, edge_gain_gr...  131 us
    psum x1, blocking collectives, on_device(): lax.psum((edge_first_grad, edge_bias_grad, edge_second_grad, edge_gain_gr...  46.1 us
    psum x1, waiting for transfers between devices, on_device(): lax.psum(matmul(edge_act, edge_second).astype(jnp.bfloat16), 'hidden')  20.5 us
    unnamed x88, local copies, waits for them, and re-layouts  12.4 us
    dot_general x8, matrix products, matmul(): return jnp.dot(lefthand, righthand, preferred_element_type=jnp.float32)  9.97 us
    dot_general x5, matrix products, matmul_tn(): lax.dot_general(lefthand, righthand, (((0,), (0,)), ((), ())), preferred_...  9.58 us
    ppermute x2, starting transfers between devices, extended(): lax.ppermute(head, axis, [((i + 1) % count, i) for i in range(count)])  7.8 us
    dot_general x4, matrix products, matmul_nt(): lax.dot_general(lefthand, righthand, (((1,), (1,)), ((), ())), preferred_...  5.78 us
  transfers between devices with their start and end apart: 8, of which 3 were waited for; matrix products, arithmetic and copies ran while one was open for 9% of the time, Pallas kernels for 0%

commit v1 on v0

v1 whole, which is shorter than its diff:
```python
import functools

import jax
import jax.numpy as jnp
from jax import lax
from jax.experimental import pallas as pl
from jax.experimental.pallas import tpu as pltpu
from jax.sharding import PartitionSpec as P

EPS = 1e-05
CHUNK = 128
F32, BF16 = jnp.float32, jnp.bfloat16
MESH = pl.DeviceIdType.MESH


def mm(lefthand, righthand):
    return jnp.dot(lefthand, righthand, preferred_element_type=F32)


def mm_tn(lefthand, righthand):
    return lax.dot_general(
        lefthand, righthand, (((0,), (0,)), ((), ())), preferred_element_type=F32
    )


def mm_nt(lefthand, righthand):
    return lax.dot_general(
        lefthand, righthand, (((1,), (1,)), ((), ())), preferred_element_type=F32
    )


def normalize(values):
    centre = values - jnp.mean(values, axis=-1, keepdims=True)
    scaled = lax.rsqrt(jnp.mean(centre * centre, axis=-1, keepdims=True) + EPS)
    return centre * scaled, scaled


def norm_back(upstream, gain, normed, scaled):
    pulled = upstream * gain
    return scaled * (
        pulled
        - jnp.mean(pulled, axis=-1, keepdims=True)
        - normed * jnp.mean(pulled * normed, axis=-1, keepdims=True)
    )


def sigmoid(values):
    return 1.0 / (1.0 + jnp.exp(-values))


class Copies:
    def __init__(self, local_sems, send_sems, recv_sems):
        self.local_sems, self.send_sems, self.recv_sems = local_sems, send_sems, recv_sems
        self.locals, self.remotes = 0, 0

    def local(self, src, dst):
        copy = pltpu.make_async_copy(src, dst, self.local_sems.at[self.locals])
        self.locals += 1
        copy.start()
        return copy

    def remote(self, src, dst, device):
        copy = pltpu.make_async_remote_copy(
            src_ref=src,
            dst_ref=dst,
            send_sem=self.send_sems.at[self.remotes],
            recv_sem=self.recv_sems.at[self.remotes],
            device_id=device,
            device_id_type=MESH,
        )
        self.remotes += 1
        copy.start()
        return copy


class Reduction:
    def __init__(self, copies, buf, landing, result, rows, steps):
        self.copies, self.buf, self.landing, self.result = copies, buf, landing, result
        self.steps = steps
        self.size = rows
        self.offset = 0
        self.land = 0
        self.trail = []
        self.flight = None

    def _rows(self, start, size):
        return pl.ds(pl.multiple_of(start, 16), size)

    def send_half(self, index):
        device, bit = self.steps[index]
        half = self.size // 2
        theirs = self.offset + (1 - bit) * half
        self.flight = self.copies.remote(
            self.buf.at[self._rows(theirs, half)],
            self.landing.at[pl.ds(self.land, half)],
            device,
        )

    def take_half(self, index):
        device, bit = self.steps[index]
        half = self.size // 2
        self.flight.wait()
        mine = self.offset + bit * half
        block = 64
        while half % block:
            block //= 2
        land = self.land
        target = self.result if index + 1 == len(self.steps) else self.buf

        def add(i, carry):
            here = pl.ds(pl.multiple_of(mine + i * block, 16), block)
            there = pl.ds(pl.multiple_of(land + i * block, 16), block)
            target[here, :] = (
                self.buf[here, :].astype(F32) + self.landing[there, :].astype(F32)
            ).astype(BF16)
            return carry

        lax.fori_loop(0, half // block, add, 0)
        self.trail.append((self.offset, self.size))
        self.offset, self.size, self.land = mine, half, land + half

    def send_own(self, index):
        device, _ = self.steps[index]
        rows = self._rows(self.offset, self.size)
        self.flight = self.copies.remote(self.result.at[rows], self.result.at[rows], device)

    def take_own(self):
        self.flight.wait()
        self.offset, self.size = self.trail.pop()


def kernel(
    sizes,
    nodes_h, edges_h, ncot_h, ecot_h, senders_v, receivers_v, lists_v,
    first_h, ebias_v, second_h, egain_v, nfirst_h, nbias_v, nsecond_h, ngain_v,
    gn_out, ge_out, ng_out, eg_out, vec_out,
    nodes, edges, ncot, ecot, w1, w2, n1, n2,
    table, outgoing, oht, oh, pre, act, normed, scales, msg, agg, nin, nact, dz, dh,
    gfirst, gfirst_send, gsecond, gsecond_send, first_in, second_in,
    spart, s_send, s_in, ge_half, ge_full, back, arriving, gnode,
    ng, n_work, n_land, eg, e_work, e_land, vec, vec_in,
    local_sems, send_sems, recv_sems,
):
    batches, patches, node_rows_padded, edge_rows_padded = sizes
    b, p, h = lax.axis_index("batch"), lax.axis_index("space"), lax.axis_index("hidden")
    other = 1 - h
    partner = (b, p, other)
    prev = (b, lax.rem(p + patches - 1, patches), h)
    after = (b, lax.rem(p + 1, patches), h)
    n_count, width = nodes.shape
    e_count = edges.shape[0]
    half = width // 2
    halo = lists_v.shape[1] // 2
    t_rows = table.shape[0]
    hid = w2.shape[0]
    hhalf = hid // 2

    def flip_space(bit_index):
        stride = 1 << bit_index
        bit = lax.rem(p // stride, 2)
        return (b, p + stride * (1 - 2 * bit), h), bit

    def flip_batch():
        return (1 - b, p, h), b

    bits = patches.bit_length() - 1
    rest = [flip_space(i) for i in range(1, bits)]
    near, far = flip_space(0), flip_batch()
    pn = p + (1 - 2 * lax.rem(p, 2))
    one = ((b * (1 - h) + (1 - b) * h, pn * (1 - h) + p * h, h), near[1] * (1 - h) + far[1] * h)
    two = (((1 - b) * (1 - h) + b * h, p * (1 - h) + pn * h, h), far[1] * (1 - h) + near[1] * h)
    steps = [one, two] + rest

    copies = Copies(local_sems, send_sems, recv_sems)
    my_rows = pl.ds(pl.multiple_of(h * e_count, 128), e_count)
    my_hidden = pl.ds(pl.multiple_of(h * hhalf, 128), hhalf)
    c_nodes = copies.local(nodes_h, nodes)
    c_w1 = copies.local(first_h, w1.at[:, my_hidden])
    c_edges = copies.local(edges_h.at[my_rows], edges)
    c_w2 = copies.local(second_h, w2.at[my_hidden])
    c_n1 = copies.local(nfirst_h, n1)
    c_n2 = copies.local(nsecond_h, n2)
    c_ncot = copies.local(ncot_h, ncot)
    c_ecot = copies.local(ecot_h.at[my_rows], ecot)

    barrier = pltpu.get_barrier_semaphore()
    friends = [partner, prev, after] + [device for device, _ in steps]
    for device in friends:
        pl.semaphore_signal(barrier, inc=1, device_id=device, device_id_type=MESH)
    c_nodes.wait()
    pick_t = (
        lax.broadcasted_iota(jnp.int32, (n_count, 2 * halo), 0) == lists_v[...]
    ).astype(BF16)
    outgoing[...] = mm_tn(pick_t, nodes[...]).astype(BF16)
    pl.semaphore_wait(barrier, len(friends))
    r_w1 = copies.remote(first_h, w1.at[:, my_hidden], partner)
    r_w2 = copies.remote(second_h, w2.at[my_hidden], partner)
    r_prev = copies.remote(
        outgoing.at[pl.ds(0, halo)], table.at[pl.ds(n_count + halo, halo)], prev
    )
    r_next = copies.remote(outgoing.at[pl.ds(halo, halo)], table.at[pl.ds(n_count, halo)], after)
    table[pl.ds(0, n_count), :] = nodes[...]
    oht[pl.ds(0, t_rows), :] = (
        lax.broadcasted_iota(jnp.int32, (t_rows, e_count), 0) == senders_v[...]
    ).astype(BF16)
    oht[pl.ds(t_rows, n_count), :] = (
        lax.broadcasted_iota(jnp.int32, (n_count, e_count), 0) == receivers_v[...]
    ).astype(BF16)
    oh[...] = oht[...].astype(F32).T.astype(BF16)

    c_w1.wait()
    c_w2.wait()
    r_w1.wait()
    p_recv = mm(nodes[...], w1[2 * width :, :]).astype(BF16)
    c_edges.wait()
    for i in range(0, e_count, CHUNK):
        rows = pl.ds(i, CHUNK)
        pre[rows, :] = (
            mm(edges[rows, :], w1[:width, :]) + mm(oh[rows, t_rows:], p_recv) + ebias_v[...]
        )
    r_prev.wait()
    r_next.wait()
    r_w2.wait()
    p_send = mm(table[...], w1[width : 2 * width, :]).astype(BF16)
    for i in range(0, e_count, CHUNK):
        rows = pl.ds(i, CHUNK)
        value = pre[rows, :] + mm(oh[rows, :t_rows], p_send)
        pre[rows, :] = value
        active = (value * sigmoid(value)).astype(BF16)
        act[rows, :] = active
        norm, scale = normalize(mm(active, w2[...]))
        normed[rows, :] = norm
        scales[rows, :] = jnp.broadcast_to(scale, (CHUNK, 128))
        msg[rows, :] = (egain_v[...] * norm).astype(BF16)
    agg[0] = mm(oht[t_rows:, :], msg[...])
    r_agg = copies.remote(agg.at[0], agg.at[1], partner)
    c_n1.wait()
    c_n2.wait()
    c_ncot.wait()
    node_half = mm(nodes[...], n1[:width, :]) + nbias_v[...]
    nin[0] = nodes[...]
    r_agg.wait()
    gathered = (agg[0] + agg[1]).astype(BF16)
    nin[1] = gathered

    n_pre = node_half + mm(gathered, n1[width:, :])
    n_sig = sigmoid(n_pre)
    n_active = (n_pre * n_sig).astype(BF16)
    nact[...] = n_active
    n_norm, n_scale = normalize(mm(n_active, n2[...]))
    n_up = ncot[...].astype(F32)
    first_core = (1 - h).astype(F32)
    vec[...] = jnp.zeros_like(vec)
    vec[3:4, :] = jnp.sum(n_up * n_norm, axis=0, keepdims=True) * first_core
    n_dz = norm_back(n_up, ngain_v[...], n_norm, n_scale).astype(BF16)
    n_slope = n_sig * (1.0 + n_pre * (1.0 - n_sig))
    n_dh = (mm_nt(n_dz, n2[...]) * n_slope).astype(BF16)
    vec[2:3, :] = jnp.sum(n_dh.astype(F32), axis=0, keepdims=True) * first_core
    agg_grad = mm_nt(n_dh, n1[width:, :]).astype(BF16)
    my_feat = pl.ds(pl.multiple_of(h * half, 128), half)
    gnode[...] = ncot[:, my_feat].astype(F32) + mm_nt(n_dh, n1[my_feat, :])
    ngh = n_work
    grad = mm_tn(nin[h], n_dh).astype(BF16)
    for j in range(2):
        ngh[pl.ds(j * width, width), :] = grad[:, j * half : (j + 1) * half]
    grad = mm_tn(nact[:, my_hidden], n_dz).astype(BF16)
    for j in range(2):
        ngh[pl.ds(2 * width + j * hhalf, hhalf), :] = grad[:, j * half : (j + 1) * half]
    filled = 2 * width + 2 * hhalf
    if node_rows_padded > filled:
        ngh[pl.ds(filled, node_rows_padded - filled), :] = jnp.zeros(
            (node_rows_padded - filled, half), BF16
        )
    node_red = Reduction(copies, n_work, n_land, ng.at[h], node_rows_padded, steps)
    node_red.send_half(0)

    c_ecot.wait()
    gain_sum = jnp.zeros((1, width), F32)
    bias_sum = jnp.zeros((1, hid), F32)
    for i in range(0, e_count, CHUNK):
        rows = pl.ds(i, CHUNK)
        upstream = ecot[rows, :].astype(F32)
        norm = normed[rows, :]
        grad = upstream + mm(oh[rows, t_rows:], agg_grad)
        gain_sum = gain_sum + jnp.sum(grad * norm, axis=0, keepdims=True)
        d_z = norm_back(grad, egain_v[...], norm, scales[rows, 0:1]).astype(BF16)
        dz[rows, :] = d_z
        value = pre[rows, :]
        s = sigmoid(value)
        d_h = (mm_nt(d_z, w2[...]) * (s * (1.0 + value * (1.0 - s)))).astype(BF16)
        dh[rows, :] = d_h
        bias_sum = bias_sum + jnp.sum(d_h.astype(F32), axis=0, keepdims=True)
    vec[0:1, :] = bias_sum
    vec[1:2, :] = gain_sum
    r_vec = copies.remote(vec, vec_in.at[0], partner)
    spart[...] = mm(oht[...], dh[...])
    s_send[...] = spart[...].astype(BF16)
    r_s = copies.remote(s_send, s_in, partner)
    grad = mm_tn(edges[...], dh[...])
    for j in range(2):
        gfirst[j] = grad[:, j * hhalf : (j + 1) * hhalf]
    gfirst_send[...] = gfirst[other].astype(BF16)
    r_first = copies.remote(gfirst_send, first_in, partner)
    gsecond[...] = mm_tn(act[...], dz[...])
    gsecond_send[...] = gsecond[pl.ds(pl.multiple_of(other * hhalf, 128), hhalf), :].astype(BF16)
    r_second = copies.remote(gsecond_send, second_in, partner)

    node_red.take_half(0)
    node_red.send_half(1)

    r_s.wait()
    spart[...] = spart[...] + s_in[...].astype(F32)
    s_all = spart[...].astype(BF16)
    t_grad = mm_nt(s_all[:t_rows], w1[pl.ds(pl.multiple_of(width + h * half, 128), half), :])
    back[...] = t_grad[n_count:].astype(BF16)
    r_back_prev = copies.remote(
        back.at[pl.ds(0, halo)], arriving.at[pl.ds(halo, halo)], prev
    )
    r_back_next = copies.remote(
        back.at[pl.ds(halo, halo)], arriving.at[pl.ds(0, halo)], after
    )
    gnode[...] = (
        gnode[...]
        + t_grad[:n_count]
        + mm_nt(s_all[t_rows:], w1[pl.ds(pl.multiple_of(2 * width + h * half, 128), half), :])
    )
    s_mine = spart[:, my_hidden].astype(BF16)
    e_work[pl.ds(width, width), :] = mm_tn(table[...], s_mine[:t_rows]).astype(BF16)
    e_work[pl.ds(2 * width, width), :] = mm_tn(nodes[...], s_mine[t_rows:]).astype(BF16)
    r_first.wait()
    e_work[pl.ds(0, width), :] = (gfirst[h] + first_in[...].astype(F32)).astype(BF16)
    r_second.wait()
    grad = (gsecond[my_hidden, :] + second_in[...].astype(F32)).astype(BF16)
    for j in range(2):
        e_work[pl.ds(3 * width + j * hhalf, hhalf), :] = grad[:, j * half : (j + 1) * half]
    filled = 3 * width + 2 * hhalf
    if edge_rows_padded > filled:
        e_work[pl.ds(filled, edge_rows_padded - filled), :] = jnp.zeros(
            (edge_rows_padded - filled, half), BF16
        )
    edge_red = Reduction(copies, e_work, e_land, eg, edge_rows_padded, steps)
    edge_red.send_half(0)
    r_vec.wait()
    vec[...] = vec[...] + vec_in[0]

    for i in range(0, e_count, CHUNK):
        rows = pl.ds(i, CHUNK)
        own = (ecot[rows, :].astype(F32) + mm_nt(dh[rows, :], w1[:width, :])).astype(BF16)
        for j in range(2):
            ge_half[j, rows, :] = own[:, j * half : (j + 1) * half]
    r_ge = copies.remote(ge_half.at[other], ge_full.at[my_rows], partner)
    c_ge = copies.local(ge_half.at[h], ge_full.at[my_rows])
    r_back_prev.wait()
    r_back_next.wait()
    gnode[...] = gnode[...] + mm(pick_t, arriving[...])
    back_out = gnode[...].astype(BF16)
    outgoing[:, :half] = back_out
    c_gn = copies.local(outgoing.at[:, pl.ds(0, half)], gn_out)
    r_ge.wait()
    c_ge.wait()
    c_geo = copies.local(ge_full, ge_out)

    count = len(steps)
    r_vec = copies.remote(vec, vec_in.at[1], steps[0][0])
    for k in range(count):
        if k > 0:
            node_red.take_half(k)
            if k + 1 < count:
                node_red.send_half(k + 1)
            else:
                node_red.send_own(count - 1)
        edge_red.take_half(k)
        r_vec.wait()
        vec[...] = vec[...] + vec_in[k + 1]
        if k + 1 < count:
            edge_red.send_half(k + 1)
            r_vec = copies.remote(vec, vec_in.at[k + 2], steps[k + 1][0])
        else:
            edge_red.send_own(count - 1)
    c_vec = copies.local(vec, vec_out)
    for k in reversed(range(count)):
        node_red.take_own()
        if k > 0:
            node_red.send_own(k - 1)
        else:
            r_node = copies.remote(ng.at[h], ng.at[h], partner)
        edge_red.take_own()
        if k > 0:
            edge_red.send_own(k - 1)
    c_eg = copies.local(eg, eg_out)
    r_node.wait()
    c_ng = copies.local(ng, ng_out)
    for copy in (c_gn, c_geo, c_vec, c_eg, c_ng):
        copy.wait()


def on_device(
    mesh_sizes, nodes, edges, node_cotangent, edge_cotangent, senders, receivers, send_lists,
    edge_first, edge_bias, edge_second, edge_gain, node_first, node_bias, node_second, node_gain,
):
    batches, patches = mesh_sizes
    group = batches * patches
    n_count, width = nodes.shape[1:]
    e_all = edges.shape[1]
    e_count = e_all // 2
    hid = 2 * edge_second.shape[0]
    half, hhalf = width // 2, hid // 2
    halo = send_lists.shape[2]
    t_rows = n_count + 2 * halo
    unit = 16 * group
    n_rows = -(-(2 * width + 2 * hhalf) // unit) * unit
    e_rows = -(-(3 * width + 2 * hhalf) // unit) * unit
    part = lax.axis_index("hidden")
    steps = group.bit_length() - 1
    own_ids = lambda ids: lax.dynamic_slice_in_dim(ids, part * e_count, e_count, 0)[None]
    row = lambda vector: vector[None, :]
    bias_all = lax.all_gather(edge_bias, "hidden", axis=0, tiled=True)
    anywhere = pl.BlockSpec(memory_space=pl.ANY)
    inside = pl.BlockSpec(memory_space=pltpu.VMEM)
    V = pltpu.VMEM
    outs = pl.pallas_call(
        functools.partial(kernel, (batches, patches, n_rows, e_rows)),
        out_shape=(
            jax.ShapeDtypeStruct((n_count, half), BF16),
            jax.ShapeDtypeStruct((e_all, half), BF16),
            jax.ShapeDtypeStruct((2, n_rows, half), BF16),
            jax.ShapeDtypeStruct((e_rows, half), BF16),
            jax.ShapeDtypeStruct((8, width), F32),
        ),
        in_specs=[
            anywhere, anywhere, anywhere, anywhere, inside, inside, inside,
            anywhere, inside, anywhere, inside, anywhere, inside, anywhere, inside,
        ],
        out_specs=(anywhere,) * 5,
        scratch_shapes=[
            V((n_count, width), BF16),
            V((e_count, width), BF16),
            V((n_count, width), BF16),
            V((e_count, width), BF16),
            V((3 * width, hid), BF16),
            V((hid, width), BF16),
            V((2 * width, hid), BF16),
            V((hid, width), BF16),
            V((t_rows, width), BF16),
            V((2 * halo, width), BF16),
            V((t_rows + n_count, e_count), BF16),
            V((e_count, t_rows + n_count), BF16),
            V((e_count, hid), F32),
            V((e_count, hid), BF16),
            V((e_count, width), F32),
            V((e_count, 128), F32),
            V((e_count, width), BF16),
            V((2, n_count, width), F32),
            V((2, n_count, width), BF16),
            V((n_count, hid), BF16),
            V((e_count, width), BF16),
            V((e_count, hid), BF16),
            V((2, width, hhalf), F32),
            V((width, hhalf), BF16),
            V((hid, width), F32),
            V((hhalf, width), BF16),
            V((width, hhalf), BF16),
            V((hhalf, width), BF16),
            V((t_rows + n_count, hid), F32),
            V((t_rows + n_count, hid), BF16),
            V((t_rows + n_count, hid), BF16),
            V((2, e_count, half), BF16),
            V((e_all, half), BF16),
            V((2 * halo, half), BF16),
            V((2 * halo, half), BF16),
            V((n_count, half), F32),
            V((2, n_rows, half), BF16),
            V((n_rows, half), BF16),
            V((n_rows, half), BF16),
            V((e_rows, half), BF16),
            V((e_rows, half), BF16),
            V((e_rows, half), BF16),
            V((8, width), F32),
            V((steps + 1, 8, width), F32),
            pltpu.SemaphoreType.DMA((16,)),
            pltpu.SemaphoreType.DMA((16 + 5 * steps,)),
            pltpu.SemaphoreType.DMA((16 + 5 * steps,)),
        ],
        compiler_params=pltpu.CompilerParams(
            collective_id=0, has_side_effects=True, vmem_limit_bytes=60 * 1024 * 1024
        ),
    )(
        nodes[0], edges[0], node_cotangent[0], edge_cotangent[0],
        own_ids(senders), own_ids(receivers), send_lists.reshape(1, -1),
        edge_first, row(bias_all), edge_second, row(edge_gain),
        node_first, row(node_bias), node_second, row(node_gain),
    )
    g_nodes, g_edges, g_node, g_edge, vec = outs
    side = lambda rows: jnp.concatenate(jnp.split(rows, 2, axis=0), axis=1)
    g_node_first = jnp.concatenate([side(g_node[j, : 2 * width]) for j in range(2)], axis=0)
    g_node_second = jnp.concatenate(
        [side(g_node[j, 2 * width : 2 * width + 2 * hhalf]) for j in range(2)], axis=0
    )
    return (
        g_nodes[None],
        g_edges[None],
        g_edge[: 3 * width].astype(F32),
        lax.dynamic_slice_in_dim(vec[0], part * hhalf, hhalf, 0),
        side(g_edge[3 * width : 3 * width + 2 * hhalf]).astype(F32),
        vec[1],
        g_node_first.astype(F32),
        vec[2],
        g_node_second.astype(F32),
        vec[3],
    )


def solution(mesh):
    placed = (
        P("batch", "space", None), P("batch", "space", None),
        P("batch", "space", None), P("batch", "space", None),
        P("space"), P("space"), P("space", None, None),
        P(None, "hidden"), P("hidden"), P("hidden", None),
        P(), P(), P(), P(), P(),
    )
    batches, patches = mesh.shape["batch"], mesh.shape["space"]
    assert mesh.shape["hidden"] == 2 and batches == 2
    assert patches & (patches - 1) == 0
    return jax.shard_map(
        functools.partial(on_device, (batches, patches)),
        mesh=mesh,
        in_specs=placed,
        out_specs=(
            P("batch", "space", "hidden"), P("batch", "space", "hidden"),
            P(None, "hidden"), P("hidden"), P("hidden", None),
            P(), P(), P(), P(), P(),
        ),
        check_vma=False,
    )
```

time: 281 us -> 95.5 us (0.34)
  waiting for transfers between devices: 152 us -> 0 us
  Pallas kernels: 0 us -> 76.5 us
  blocking collectives: 46.1 us -> 3.38 us
  matrix products: 29.2 us -> 0 us
  starting transfers between devices: 15.4 us -> 0 us
  between operations: 14.3 us -> 0.7 us
  local copies, waits for them, and re-layouts: 16.2 us -> 8.51 us
    psum x2 -> x0, waiting for transfers between devices: 152 us -> none  [the longest x1 131 us: on_device(): lax.psum((edge_first_grad, edge_bias_grad, edge_second_grad, edge_gain_gr...]
    pallas_call x0 -> x1, Pallas kernels: none -> 76.5 us  [on_device(): pl.pallas_call(functools.partial(kernel, (batches, patches, n_rows, e_row...]
    psum x1 -> x0, blocking collectives: 46.1 us -> none  [on_device(): lax.psum((edge_first_grad, edge_bias_grad, edge_second_grad, edge_gain_gr...]
    dot_general x20 -> x0, matrix products: 29.2 us -> none  [the longest x8 9.97 us: matmul(): return jnp.dot(lefthand, righthand, preferred_element_type=jnp.float32)]
    unnamed x88 -> x8, local copies, waits for them, and re-layouts: 12.4 us -> 1.44 us
    ppermute x4 -> x0, starting transfers between devices: 10.9 us -> none  [the longest x2 7.8 us: extended(): lax.ppermute(head, axis, [((i + 1) % count, i) for i in range(count)])]
    all_to_all x1 -> x0, starting transfers between devices: 4.44 us -> none  [on_device(): lax.all_to_all(blocks, 'hidden', split_axis=1, concat_axis=3, tiled=True)]
    reduce_sum x4 -> x0, other arithmetic: 3.6 us -> none  [the longest x2 1.86 us: normalize(): scaled = lax.rsqrt(jnp.mean(centre * centre, axis=-1, keepdims=True) + EPS)]
  transfers between devices with their start and end apart: 8 -> 0, of which waited for: 3 -> 0; matrix products, arithmetic and copies ran while one was open for 9% -> 0% of each run, Pallas kernels for 0% -> 0%
where the time goes in v1:
time: 95.5 us; the launch traced here: 95.1 us
  Pallas kernels  76.5 us (80%)
  local copies, waits for them, and re-layouts  8.51 us (9%)
  other arithmetic  5.95 us (6%)
  blocking collectives  3.38 us (4%)
    pallas_call x1, Pallas kernels, on_device(): pl.pallas_call(functools.partial(kernel, (batches, patches, n_rows, e_row...  76.5 us
    all_gather x1, blocking collectives, on_device(): bias_all = lax.all_gather(edge_bias, 'hidden', axis=0, tiled=True)  3.38 us
    dynamic_slice x2, local copies, waits for them, and re-layouts, on_device(): lax.dynamic_slice_in_dim(ids, part * e_count, e_count, 0)[None]  2.67 us
    convert_element_type x1, other arithmetic, on_device(): g_edge[:3 * width].astype(F32)  2.39 us

profile of v1, /device:TPU:0, one launch (start us, length us, event | category | flops | bytes accessed | tf_op | source)
XLA Modules:
  0.0 95.1 jit_solution(7469578770328159345)
XLA Ops:
  0.6 1.3 %reshape.32.lists_v = s32[1,128]{1,0:T(1,128)} reshape(s32[1,2,64]{2,1,0:T(2,128)} %param.21) | data formatting | bytes 1024 | tf_op jit(solution)/shard_map/reshape | solution.py:489
  1.9 1.3 %dynamic_slice.11 = s32[512]{0:T(512)} dynamic-slice(s32[1024]{0:T(1024)} %param.19, s32[]{:T(128)S(6)} %select_n.7), dynamic_slice_sizes={512} | dynamic-slice | bytes 4100 | tf_op jit(solution)/shard_map/dynamic_slice | solution.py:415
  3.3 1.3 %dynamic_slice.12 = s32[512]{0:T(512)} dynamic-slice(s32[1024]{0:T(1024)} %param.20, s32[]{:T(128)S(6)} %select_n.7), dynamic_slice_sizes={512} | dynamic-slice | bytes 4100 | tf_op jit(solution)/shard_map/dynamic_slice | solution.py:415
  4.6 3.4 %all-gather = f32[2,1,256]{2,1,0:T(1,128)} all-gather(f32[1,1,256]{2,1,0:T(1,128)} %bitcast.48), channel_id=1, replica_groups=mesh['batch'=2,'space'=8,'hidden'=2] {'hidden'}, dimensions={0}, use_global_device_ids=true | all-gather | bytes 3072 | tf_op jit(solution)/shard_map/all_gather | solution.py:417
  8.0 76.5 %shard_map.222 = (bf16[128,256]{1,0:T(8,128)(2,1)}, bf16[1024,256]{1,0:T(8,128)(2,1)}, bf16[2,1536,256]{2,1,0:T(8,128)(2,1)}, bf16[2048,256]{1,0:T(8,128)(2,1)}, f32[8,512]{1,0:T(8,128)}) custom-call(bf16[128,512]{1,0:T(8,128)(2,1)} %bitcast.36, bf16[1024,512]{1,0:T(8,128)(2,1)} %bitcast.33, bf16[128,512]{1,0:T(8,128)(2,1)} %bitcast.37, ...), custom_call_target="tpu_custom_call" | custom-call | tf_op jit(solution)/shard_map/pallas_call | solution.py:421
  84.5 0.0 copy-start
  84.5 1.5 %fusion.1 = (f32[1,512]{1,0:T(1,128)}, f32[1,512]{1,0:T(1,128)}, f32[1,512]{1,0:T(1,128)}, f32[1,512]{1,0:T(1,128)S(1)}) fusion(f32[8,512]{1,0:T(8,128)} %get-tuple-element.18), kind=kLoop, calls=%fused_computation.14 | loop fusion | bytes 16384 | tf_op jit(solution)/shard_map/slice | solution.py:509
  86.0 0.6 constant_dynamic-slice_fusion
  86.6 1.0 %fusion = (bf16[256,256]{1,0:T(8,128)(2,1)S(1)}, bf16[256,256]{1,0:T(8,128)(2,1)S(1)}) fusion(bf16[2048,256]{1,0:T(8,128)(2,1)} %get-tuple-element.17), kind=kLoop, calls=%fused_computation.13 | loop fusion | bytes 524288 | tf_op jit(solution)/shard_map/split | solution.py:494
  87.6 0.9 maximum_convert_fusion.2
  88.4 2.4 %slice_convert_fusion = f32[1536,256]{1,0:T(8,128)} fusion(bf16[2048,256]{1,0:T(8,128)(2,1)} %get-tuple-element.17), kind=kLoop, calls=%fused_computation.1 | loop fusion | flops 393216 | bytes 2359296 | tf_op jit(solution)/shard_map/convert_element_type | solution.py:502
  90.8 0.0 copy-done
  90.8 0.1 slice_bitcast_fusion.3
  90.9 0.0 copy-start.2
  90.9 0.0 copy-start.1
  90.9 1.1 %maximum_convert_fusion.1 = f32[512,512]{1,0:T(8,128)} fusion(bf16[256,256]{1,0:T(8,128)(2,1)S(1)} %get-tuple-element.21, bf16[256,256]{1,0:T(8,128)(2,1)S(1)} %get-tuple-element.22, bf16[256,256]{1,0:T(8,128)(2,1)S(1)} %get-tuple-element.23, bf16[256,256]{1,0:T(8,128)(2,1)S(1)} %get-tuple-element.20), kind=kLoop, calls=%fused_computation.2 | loop fusion | flops 2097152 | bytes 1572864 | tf_op jit(solution)/shard_map/convert_element_type | solution.py:508
  92.0 1.6 %maximum_convert_fusion = f32[1024,512]{1,0:T(8,128)} fusion(bf16[512,256]{1,0:T(8,128)(2,1)S(1)} %get-tuple-element.25, bf16[512,256]{1,0:T(8,128)(2,1)S(1)} %get-tuple-element.26, bf16[512,256]{1,0:T(8,128)(2,1)S(1)} %get-tuple-element.27, bf16[512,256]{1,0:T(8,128)(2,1)S(1)} %get-tuple-element.24), kind=kLoop, calls=%fused_computation | loop fusion | flops 4194304 | bytes 3145728 | tf_op jit(solution)/shard_map/convert_element_type | solution.py:506
  93.6 0.0 copy-done.2
  93.7 0.6 copy.27
  94.3 0.0 copy-done.1
  94.3 0.8 copy.28
  (1 shorter events, 0.0 us)
Async XLA Ops:
  84.5 6.3 %copy-start = (bf16[2,1536,256]{2,1,0:T(8,128)(2,1)S(1)}, bf16[2,1536,256]{2,1,0:T(8,128)(2,1)}, u32[]{:S(2)}) copy-start(bf16[2,1536,256]{2,1,0:T(8,128)(2,1)} %get-tuple-element.19) | copy-start | bytes 4718596
  90.9 2.7 %copy-start.2 = (bf16[128,256]{1,0:T(8,128)(2,1)S(1)}, bf16[128,256]{1,0:T(8,128)(2,1)}, u32[]{:S(2)}) copy-start(bf16[128,256]{1,0:T(8,128)(2,1)} %get-tuple-element.15) | copy-start | bytes 196612
  90.9 3.4 %copy-start.1 = (bf16[1024,256]{1,0:T(8,128)(2,1)S(1)}, bf16[1024,256]{1,0:T(8,128)(2,1)}, u32[]{:S(2)}) copy-start(bf16[1024,256]{1,0:T(8,128)(2,1)} %get-tuple-element.16) | copy-start | bytes 1572868

commit v2 on v1

--- a/solution.py
+++ b/solution.py
@@ -8,7 +8,7 @@
 from jax.sharding import PartitionSpec as P
 
 EPS = 1e-05
-CHUNK = 128
+CHUNK = 256
 F32, BF16 = jnp.float32, jnp.bfloat16
 MESH = pl.DeviceIdType.MESH
 
@@ -82,6 +82,8 @@
         self.land = 0
         self.trail = []
         self.flight = None
+        self.stage = 0
+        self.done = False
 
     def _rows(self, start, size):
         return pl.ds(pl.multiple_of(start, 16), size)
@@ -118,6 +120,24 @@
         lax.fori_loop(0, half // block, add, 0)
         self.trail.append((self.offset, self.size))
         self.offset, self.size, self.land = mine, half, land + half
+        self.stage += 1
+
+    def advance(self):
+        count = len(self.steps)
+        if self.done:
+            return
+        if self.stage < count:
+            self.take_half(self.stage)
+            if self.stage < count:
+                self.send_half(self.stage)
+            else:
+                self.send_own(count - 1)
+        else:
+            self.take_own()
+            if self.stage < 2 * count:
+                self.send_own(2 * count - 1 - self.stage)
+            else:
+                self.done = True
 
     def send_own(self, index):
         device, _ = self.steps[index]
@@ -127,6 +147,7 @@
     def take_own(self):
         self.flight.wait()
         self.offset, self.size = self.trail.pop()
+        self.stage += 1
 
 
 def kernel(
@@ -138,7 +159,7 @@
     table, outgoing, oht, oh, pre, act, normed, scales, msg, agg, nin, nact, dz, dh,
     gfirst, gfirst_send, gsecond, gsecond_send, first_in, second_in,
     spart, s_send, s_in, ge_half, ge_full, back, arriving, gnode,
-    ng, n_work, n_land, eg, e_work, e_land, vec, vec_in,
+    ng, n_work, n_land, eg, top, top_land, low, low_land, vec, vec_in, bias,
     local_sems, send_sems, recv_sems,
 ):
     batches, patches, node_rows_padded, edge_rows_padded = sizes
@@ -150,7 +171,7 @@
     n_count, width = nodes.shape
     e_count = edges.shape[0]
     half = width // 2
-    halo = lists_v.shape[1] // 2
+    halo = lists_v.shape[1]
     t_rows = table.shape[0]
     hid = w2.shape[0]
     hhalf = hid // 2
@@ -170,6 +191,12 @@
     one = ((b * (1 - h) + (1 - b) * h, pn * (1 - h) + p * h, h), near[1] * (1 - h) + far[1] * h)
     two = (((1 - b) * (1 - h) + b * h, p * (1 - h) + pn * h, h), far[1] * (1 - h) + near[1] * h)
     steps = [one, two] + rest
+
+    def clear(ref, filled):
+        if ref.shape[0] > filled:
+            ref[pl.ds(filled, ref.shape[0] - filled), :] = jnp.zeros(
+                (ref.shape[0] - filled, half), BF16
+            )
 
     copies = Copies(local_sems, send_sems, recv_sems)
     my_rows = pl.ds(pl.multiple_of(h * e_count, 128), e_count)
@@ -188,11 +215,13 @@
     for device in friends:
         pl.semaphore_signal(barrier, inc=1, device_id=device, device_id_type=MESH)
     c_nodes.wait()
-    pick_t = (
-        lax.broadcasted_iota(jnp.int32, (n_count, 2 * halo), 0) == lists_v[...]
-    ).astype(BF16)
-    outgoing[...] = mm_tn(pick_t, nodes[...]).astype(BF16)
+    lines = lax.broadcasted_iota(jnp.int32, (n_count, halo), 0)
+    pick_t = [(lines == lists_v[j : j + 1, :]).astype(BF16) for j in range(2)]
+    for j in range(2):
+        outgoing[pl.ds(j * halo, halo), :] = mm_tn(pick_t[j], nodes[...]).astype(BF16)
     pl.semaphore_wait(barrier, len(friends))
+    r_bias = copies.remote(ebias_v, bias.at[:, my_hidden], partner)
+    bias[:, my_hidden] = ebias_v[...]
     r_w1 = copies.remote(first_h, w1.at[:, my_hidden], partner)
     r_w2 = copies.remote(second_h, w2.at[my_hidden], partner)
     r_prev = copies.remote(
@@ -201,22 +230,23 @@
     r_next = copies.remote(outgoing.at[pl.ds(halo, halo)], table.at[pl.ds(n_count, halo)], after)
     table[pl.ds(0, n_count), :] = nodes[...]
     oht[pl.ds(0, t_rows), :] = (
-        lax.broadcasted_iota(jnp.int32, (t_rows, e_count), 0) == senders_v[...]
+        lax.broadcasted_iota(jnp.int32, (t_rows, e_count), 0) == senders_v[:, my_rows]
     ).astype(BF16)
     oht[pl.ds(t_rows, n_count), :] = (
-        lax.broadcasted_iota(jnp.int32, (n_count, e_count), 0) == receivers_v[...]
+        lax.broadcasted_iota(jnp.int32, (n_count, e_count), 0) == receivers_v[:, my_rows]
     ).astype(BF16)
     oh[...] = oht[...].astype(F32).T.astype(BF16)
 
     c_w1.wait()
     c_w2.wait()
     r_w1.wait()
+    r_bias.wait()
     p_recv = mm(nodes[...], w1[2 * width :, :]).astype(BF16)
     c_edges.wait()
     for i in range(0, e_count, CHUNK):
         rows = pl.ds(i, CHUNK)
         pre[rows, :] = (
-            mm(edges[rows, :], w1[:width, :]) + mm(oh[rows, t_rows:], p_recv) + ebias_v[...]
+            mm(edges[rows, :], w1[:width, :]) + mm(oh[rows, t_rows:], p_recv) + bias[...]
         )
     r_prev.wait()
     r_next.wait()
@@ -266,11 +296,7 @@
     grad = mm_tn(nact[:, my_hidden], n_dz).astype(BF16)
     for j in range(2):
         ngh[pl.ds(2 * width + j * hhalf, hhalf), :] = grad[:, j * half : (j + 1) * half]
-    filled = 2 * width + 2 * hhalf
-    if node_rows_padded > filled:
-        ngh[pl.ds(filled, node_rows_padded - filled), :] = jnp.zeros(
-            (node_rows_padded - filled, half), BF16
-        )
+    clear(ngh, 2 * width + 2 * hhalf)
     node_red = Reduction(copies, n_work, n_land, ng.at[h], node_rows_padded, steps)
     node_red.send_half(0)
 
@@ -293,9 +319,6 @@
     vec[0:1, :] = bias_sum
     vec[1:2, :] = gain_sum
     r_vec = copies.remote(vec, vec_in.at[0], partner)
-    spart[...] = mm(oht[...], dh[...])
-    s_send[...] = spart[...].astype(BF16)
-    r_s = copies.remote(s_send, s_in, partner)
     grad = mm_tn(edges[...], dh[...])
     for j in range(2):
         gfirst[j] = grad[:, j * hhalf : (j + 1) * hhalf]
@@ -304,9 +327,20 @@
     gsecond[...] = mm_tn(act[...], dz[...])
     gsecond_send[...] = gsecond[pl.ds(pl.multiple_of(other * hhalf, 128), hhalf), :].astype(BF16)
     r_second = copies.remote(gsecond_send, second_in, partner)
-
-    node_red.take_half(0)
-    node_red.send_half(1)
+    spart[...] = mm(oht[...], dh[...])
+    s_send[...] = spart[...].astype(BF16)
+    r_s = copies.remote(s_send, s_in, partner)
+    node_red.advance()
+    r_first.wait()
+    top[pl.ds(0, width), :] = (gfirst[h] + first_in[...].astype(F32)).astype(BF16)
+    r_second.wait()
+    grad = (gsecond[my_hidden, :] + second_in[...].astype(F32)).astype(BF16)
+    for j in range(2):
+        top[pl.ds(width + j * hhalf, hhalf), :] = grad[:, j * half : (j + 1) * half]
+    clear(top, width + 2 * hhalf)
+    top_red = Reduction(copies, top, top_land, eg.at[0], edge_rows_padded, steps)
+    top_red.send_half(0)
+    node_red.advance()
 
     r_s.wait()
     spart[...] = spart[...] + s_in[...].astype(F32)
@@ -325,23 +359,16 @@
         + mm_nt(s_all[t_rows:], w1[pl.ds(pl.multiple_of(2 * width + h * half, 128), half), :])
     )
     s_mine = spart[:, my_hidden].astype(BF16)
-    e_work[pl.ds(width, width), :] = mm_tn(table[...], s_mine[:t_rows]).astype(BF16)
-    e_work[pl.ds(2 * width, width), :] = mm_tn(nodes[...], s_mine[t_rows:]).astype(BF16)
-    r_first.wait()
-    e_work[pl.ds(0, width), :] = (gfirst[h] + first_in[...].astype(F32)).astype(BF16)
-    r_second.wait()
-    grad = (gsecond[my_hidden, :] + second_in[...].astype(F32)).astype(BF16)
-    for j in range(2):
-        e_work[pl.ds(3 * width + j * hhalf, hhalf), :] = grad[:, j * half : (j + 1) * half]
-    filled = 3 * width + 2 * hhalf
-    if edge_rows_padded > filled:
-        e_work[pl.ds(filled, edge_rows_padded - filled), :] = jnp.zeros(
-            (edge_rows_padded - filled, half), BF16
-        )
-    edge_red = Reduction(copies, e_work, e_land, eg, edge_rows_padded, steps)
-    edge_red.send_half(0)
+    low[pl.ds(0, width), :] = mm_tn(table[...], s_mine[:t_rows]).astype(BF16)
+    low[pl.ds(width, width), :] = mm_tn(nodes[...], s_mine[t_rows:]).astype(BF16)
+    clear(low, 2 * width)
+    low_red = Reduction(copies, low, low_land, eg.at[1], edge_rows_padded, steps)
+    low_red.send_half(0)
+    node_red.advance()
     r_vec.wait()
     vec[...] = vec[...] + vec_in[0]
+    count = len(steps)
+    r_node = None
 
     for i in range(0, e_count, CHUNK):
         rows = pl.ds(i, CHUNK)
@@ -352,7 +379,9 @@
     c_ge = copies.local(ge_half.at[h], ge_full.at[my_rows])
     r_back_prev.wait()
     r_back_next.wait()
-    gnode[...] = gnode[...] + mm(pick_t, arriving[...])
+    gnode[...] = gnode[...] + (
+        mm(pick_t[0], arriving[:halo]) + mm(pick_t[1], arriving[halo:])
+    )
     back_out = gnode[...].astype(BF16)
     outgoing[:, :half] = back_out
     c_gn = copies.local(outgoing.at[:, pl.ds(0, half)], gn_out)
@@ -360,33 +389,24 @@
     c_ge.wait()
     c_geo = copies.local(ge_full, ge_out)
 
-    count = len(steps)
     r_vec = copies.remote(vec, vec_in.at[1], steps[0][0])
+    top_red.advance()
+    low_red.advance()
     for k in range(count):
-        if k > 0:
-            node_red.take_half(k)
-            if k + 1 < count:
-                node_red.send_half(k + 1)
-            else:
-                node_red.send_own(count - 1)
-        edge_red.take_half(k)
         r_vec.wait()
         vec[...] = vec[...] + vec_in[k + 1]
         if k + 1 < count:
-            edge_red.send_half(k + 1)
             r_vec = copies.remote(vec, vec_in.at[k + 2], steps[k + 1][0])
-        else:
-            edge_red.send_own(count - 1)
+        node_red.advance()
+        top_red.advance()
+        low_red.advance()
     c_vec = copies.local(vec, vec_out)
-    for k in reversed(range(count)):
-        node_red.take_own()
-        if k > 0:
-            node_red.send_own(k - 1)
-        else:
+    while not (node_red.done and top_red.done and low_red.done):
+        node_red.advance()
+        if node_red.done and r_node is None:
             r_node = copies.remote(ng.at[h], ng.at[h], partner)
-        edge_red.take_own()
-        if k > 0:
-            edge_red.send_own(k - 1)
+        top_red.advance()
+        low_red.advance()
     c_eg = copies.local(eg, eg_out)
     r_node.wait()
     c_ng = copies.local(ng, ng_out)
@@ -409,12 +429,10 @@
     t_rows = n_count + 2 * halo
     unit = 16 * group
     n_rows = -(-(2 * width + 2 * hhalf) // unit) * unit
-    e_rows = -(-(3 * width + 2 * hhalf) // unit) * unit
+    e_rows = -(-max(2 * width, width + 2 * hhalf) // unit) * unit
     part = lax.axis_index("hidden")
     steps = group.bit_length() - 1
-    own_ids = lambda ids: lax.dynamic_slice_in_dim(ids, part * e_count, e_count, 0)[None]
     row = lambda vector: vector[None, :]
-    bias_all = lax.all_gather(edge_bias, "hidden", axis=0, tiled=True)
     anywhere = pl.BlockSpec(memory_space=pl.ANY)
     inside = pl.BlockSpec(memory_space=pltpu.VMEM)
     V = pltpu.VMEM
@@ -424,7 +442,7 @@
             jax.ShapeDtypeStruct((n_count, half), BF16),
             jax.ShapeDtypeStruct((e_all, half), BF16),
             jax.ShapeDtypeStruct((2, n_rows, half), BF16),
-            jax.ShapeDtypeStruct((e_rows, half), BF16),
+            jax.ShapeDtypeStruct((2, e_rows, half), BF16),
             jax.ShapeDtypeStruct((8, width), F32),
         ),
         in_specs=[
@@ -472,22 +490,25 @@
             V((2, n_rows, half), BF16),
             V((n_rows, half), BF16),
             V((n_rows, half), BF16),
+            V((2, e_rows, half), BF16),
+            V((e_rows, half), BF16),
             V((e_rows, half), BF16),
             V((e_rows, half), BF16),
             V((e_rows, half), BF16),
             V((8, width), F32),
             V((steps + 1, 8, width), F32),
+            V((1, hid), F32),
             pltpu.SemaphoreType.DMA((16,)),
-            pltpu.SemaphoreType.DMA((16 + 5 * steps,)),
-            pltpu.SemaphoreType.DMA((16 + 5 * steps,)),
+            pltpu.SemaphoreType.DMA((16 + 7 * steps,)),
+            pltpu.SemaphoreType.DMA((16 + 7 * steps,)),
         ],
         compiler_params=pltpu.CompilerParams(
             collective_id=0, has_side_effects=True, vmem_limit_bytes=60 * 1024 * 1024
         ),
     )(
         nodes[0], edges[0], node_cotangent[0], edge_cotangent[0],
-        own_ids(senders), own_ids(receivers), send_lists.reshape(1, -1),
-        edge_first, row(bias_all), edge_second, row(edge_gain),
+        row(senders), row(receivers), send_lists[0],
+        edge_first, row(edge_bias), edge_second, row(edge_gain),
         node_first, row(node_bias), node_second, row(node_gain),
     )
     g_nodes, g_edges, g_node, g_edge, vec = outs
@@ -499,9 +520,9 @@
     return (
         g_nodes[None],
         g_edges[None],
-        g_edge[: 3 * width].astype(F32),
+        jnp.concatenate([g_edge[0, :width], g_edge[1, : 2 * width]], axis=0).astype(F32),
         lax.dynamic_slice_in_dim(vec[0], part * hhalf, hhalf, 0),
-        side(g_edge[3 * width : 3 * width + 2 * hhalf]).astype(F32),
+        side(g_edge[0, width : width + 2 * hhalf]).astype(F32),
         vec[1],
         g_node_first.astype(F32),
         vec[2],

time: 95.5 us -> 85.9 us (0.90)
  blocking collectives: 3.38 us -> 0 us
  Pallas kernels: 76.5 us -> 73.3 us
  local copies, waits for them, and re-layouts: 8.51 us -> 6.84 us
  other arithmetic: 5.95 us -> 4.82 us
    all_gather x1 -> x0, blocking collectives: 3.38 us -> none  [on_device(): bias_all = lax.all_gather(edge_bias, 'hidden', axis=0, tiled=True)]
    pallas_call x1, Pallas kernels: 76.5 us -> 73.3 us  [on_device(): pl.pallas_call(functools.partial(kernel, (batches, patches, n_rows, e_row...]
    dynamic_slice x2 -> x0, local copies, waits for them, and re-layouts: 2.67 us -> none  [on_device(): lax.dynamic_slice_in_dim(ids, part * e_count, e_count, 0)[None]]
    reshape x1 -> x0, local copies, waits for them, and re-layouts: 1.27 us -> none  [on_device(): send_lists.reshape(1, -1)]
    split x3 -> x2, local copies, waits for them, and re-layouts: 1.09 us -> 2.3 us  [on_device(): side = lambda rows: jnp.concatenate(jnp.split(rows, 2, axis=0), axis=1)]
    convert_element_type x2, other arithmetic: 3.25 us -> 2.11 us  [the longest x1 1.26 us: on_device(): jnp.concatenate([g_edge[0, :width], g_edge[1, :2 * width]], axis=0)]
    squeeze x0 -> x1, local copies, waits for them, and re-layouts: none -> 1.08 us  [on_device(): g_edge[1, :2 * width]]
where the time goes in v2:
time: 85.9 us; the launch traced here: 85.6 us
  Pallas kernels  73.3 us (85%)
  local copies, waits for them, and re-layouts  6.84 us (8%)
  other arithmetic  4.82 us (6%)
    pallas_call x1, Pallas kernels, on_device(): pl.pallas_call(functools.partial(kernel, (batches, patches, n_rows, e_row...  73.3 us
    split x2, local copies, waits for them, and re-layouts, on_device(): side = lambda rows: jnp.concatenate(jnp.split(rows, 2, axis=0), axis=1)  2.3 us

profile of v2, /device:TPU:0, one launch (start us, length us, event | category | flops | bytes accessed | tf_op | source)
XLA Modules:
  0.0 85.6 jit_solution(15648115600957698867)
XLA Ops:
  0.7 73.3 %shard_map.222 = (bf16[128,256]{1,0:T(8,128)(2,1)}, bf16[1024,256]{1,0:T(8,128)(2,1)}, bf16[2,1536,256]{2,1,0:T(8,128)(2,1)}, bf16[2,1024,256]{2,1,0:T(8,128)(2,1)}, f32[8,512]{1,0:T(8,128)}) custom-call(bf16[128,512]{1,0:T(8,128)(2,1)} %bitcast.44, bf16[1024,512]{1,0:T(8,128)(2,1)} %bitcast.41, bf16[128,512]{1,0:T(8,128)(2,1)} %bitcast.45, ...), custom_call_target="tpu_custom_call" | custom-call | tf_op jit(solution)/shard_map/pallas_call | solution.py:439
  73.9 0.0 copy-start
  74.0 1.5 %fusion = (f32[1,512]{1,0:T(1,128)}, f32[1,512]{1,0:T(1,128)}, f32[1,512]{1,0:T(1,128)}, f32[1,512]{1,0:T(1,128)S(1)}) fusion(f32[8,512]{1,0:T(8,128)} %get-tuple-element.18), kind=kLoop, calls=%fused_computation.17 | loop fusion | bytes 16384 | tf_op jit(solution)/shard_map/slice | solution.py:530
  75.4 0.6 constant_dynamic-slice_fusion
  76.0 1.1 %slice_bitcast_fusion = bf16[1024,256]{1,0:T(8,128)(2,1)S(1)} fusion(bf16[2,1024,256]{2,1,0:T(8,128)(2,1)} %get-tuple-element.17), kind=kLoop, calls=%fused_computation.3 | loop fusion | bytes 1048576 | tf_op jit(solution)/shard_map/squeeze | solution.py:523
  77.1 1.3 %slice_bitcast_fusion.9 = (bf16[256,256]{1,0:T(8,128)(2,1)S(1)}, bf16[256,256]{1,0:T(8,128)(2,1)S(1)}, bf16[256,256]{1,0:T(8,128)(2,1)S(1)}, bf16[256,256]{1,0:T...) fusion(bf16[2,1536,256]{2,1,0:T(8,128)(2,1)} %get-tuple-element.19, ...), kind=kLoop, calls=%fused_computation.13 | loop fusion | bytes 1572864 | tf_op jit(solution)/shard_map/split | solution.py:515
  78.3 0.0 copy-done
  78.3 1.0 %slice_bitcast_fusion.4 = (bf16[512,256]{1,0:T(8,128)(2,1)S(1)}, bf16[512,256]{1,0:T(8,128)(2,1)S(1)}, bf16[512,256]{1,0:T(8,128)(2,1)S(1)}, bf16[512,256]{1,0:T(8,128)(2,1)S(1)}, bf16[512,256]{1,0:T(8,128)(2,1)S(1)}) fusion(bf16[2,1536,256]{2,1,0:T(8,128)(2,1)S(1)} %copy-done, bf16[2,1024,256]{2,1,0:T(8,128)(2,1)} %get-tuple-element.17), kind=kLoop, calls=%fused_computation.8 | loop fusion | bytes 2621440 | tf_op jit(solution)/shard_map/split | solution.py:515
  79.4 1.1 %maximum_convert_fusion.2 = f32[512,512]{1,0:T(8,128)} fusion(bf16[256,256]{1,0:T(8,128)(2,1)S(1)} %get-tuple-element.21, bf16[256,256]{1,0:T(8,128)(2,1)S(1)} %get-tuple-element.22, bf16[256,256]{1,0:T(8,128)(2,1)S(1)} %get-tuple-element.23, bf16[256,256]{1,0:T(8,128)(2,1)S(1)} %get-tuple-element.20), kind=kLoop, calls=%fused_computation.2 | loop fusion | flops 2097152 | bytes 1572864 | tf_op jit(solution)/shard_map/convert_element_type | solution.py:529
  80.5 0.9 maximum_convert_fusion.3
  81.3 0.0 copy-start.2
  81.3 0.0 copy-start.1
  81.3 1.6 %maximum_convert_fusion = f32[1024,512]{1,0:T(8,128)} fusion(bf16[512,256]{1,0:T(8,128)(2,1)S(1)} %get-tuple-element.25, bf16[512,256]{1,0:T(8,128)(2,1)S(1)} %get-tuple-element.26, bf16[512,256]{1,0:T(8,128)(2,1)S(1)} %get-tuple-element.27, bf16[512,256]{1,0:T(8,128)(2,1)S(1)} %get-tuple-element.24), kind=kLoop, calls=%fused_computation | loop fusion | flops 4194304 | bytes 3145728 | tf_op jit(solution)/shard_map/convert_element_type | solution.py:527
  82.9 1.3 %maximum_convert_fusion.1 = f32[1536,256]{1,0:T(8,128)} fusion(bf16[1024,256]{1,0:T(8,128)(2,1)S(1)} %slice_bitcast_fusion, bf16[512,256]{1,0:T(8,128)(2,1)S(1)} %get-tuple-element.34), kind=kLoop, calls=%fused_computation.1 | loop fusion | flops 1572864 | bytes 2359296 | tf_op jit(solution)/shard_map/convert_element_type | solution.py:523
  84.2 0.0 copy-done.2
  84.2 0.6 copy.27
  84.8 0.0 copy-done.1
  84.8 0.8 copy.28
Async XLA Ops:
  73.9 4.4 %copy-start = (bf16[2,1536,256]{2,1,0:T(8,128)(2,1)S(1)}, bf16[2,1536,256]{2,1,0:T(8,128)(2,1)}, u32[]{:S(2)}) copy-start(bf16[2,1536,256]{2,1,0:T(8,128)(2,1)} %get-tuple-element.19) | copy-start | bytes 4718596
  81.3 2.9 %copy-start.2 = (bf16[128,256]{1,0:T(8,128)(2,1)S(1)}, bf16[128,256]{1,0:T(8,128)(2,1)}, u32[]{:S(2)}) copy-start(bf16[128,256]{1,0:T(8,128)(2,1)} %get-tuple-element.15) | copy-start | bytes 196612
  81.3 3.5 %copy-start.1 = (bf16[1024,256]{1,0:T(8,128)(2,1)S(1)}, bf16[1024,256]{1,0:T(8,128)(2,1)}, u32[]{:S(2)}) copy-start(bf16[1024,256]{1,0:T(8,128)(2,1)} %get-tuple-element.16) | copy-start | bytes 1572868

commit v3 on v2

--- a/solution.py
+++ b/solution.py
@@ -154,7 +154,7 @@
     sizes,
     nodes_h, edges_h, ncot_h, ecot_h, senders_v, receivers_v, lists_v,
     first_h, ebias_v, second_h, egain_v, nfirst_h, nbias_v, nsecond_h, ngain_v,
-    gn_out, ge_out, ng_out, eg_out, vec_out,
+    gn_out, ge_out, ef_out, es_out, nf_out, ns_out, vec_out,
     nodes, edges, ncot, ecot, w1, w2, n1, n2,
     table, outgoing, oht, oh, pre, act, normed, scales, msg, agg, nin, nact, dz, dh,
     gfirst, gfirst_send, gsecond, gsecond_send, first_in, second_in,
@@ -369,6 +369,7 @@
     vec[...] = vec[...] + vec_in[0]
     count = len(steps)
     r_node = None
+    c_top = []
 
     for i in range(0, e_count, CHUNK):
         rows = pl.ds(i, CHUNK)
@@ -393,24 +394,46 @@
     top_red.advance()
     low_red.advance()
     for k in range(count):
+        node_red.advance()
+        top_red.advance()
+        low_red.advance()
         r_vec.wait()
         vec[...] = vec[...] + vec_in[k + 1]
         if k + 1 < count:
             r_vec = copies.remote(vec, vec_in.at[k + 2], steps[k + 1][0])
-        node_red.advance()
-        top_red.advance()
-        low_red.advance()
     c_vec = copies.local(vec, vec_out)
     while not (node_red.done and top_red.done and low_red.done):
         node_red.advance()
         if node_red.done and r_node is None:
             r_node = copies.remote(ng.at[h], ng.at[h], partner)
         top_red.advance()
+        if top_red.done and not c_top:
+            c_top.append(copies.local(eg.at[0, pl.ds(0, width)], ef_out.at[pl.ds(0, width)]))
+            for j in range(2):
+                c_top.append(
+                    copies.local(
+                        eg.at[0, pl.ds(width + j * hhalf, hhalf)],
+                        es_out.at[:, pl.ds(j * half, half)],
+                    )
+                )
         low_red.advance()
-    c_eg = copies.local(eg, eg_out)
+    c_low = copies.local(eg.at[1, pl.ds(0, 2 * width)], ef_out.at[pl.ds(width, 2 * width)])
     r_node.wait()
-    c_ng = copies.local(ng, ng_out)
-    for copy in (c_gn, c_geo, c_vec, c_eg, c_ng):
+    for q in range(2):
+        for j in range(2):
+            c_top.append(
+                copies.local(
+                    ng.at[q, pl.ds(j * width, width)],
+                    nf_out.at[pl.ds(q * width, width), pl.ds(j * half, half)],
+                )
+            )
+            c_top.append(
+                copies.local(
+                    ng.at[q, pl.ds(2 * width + j * hhalf, hhalf)],
+                    ns_out.at[pl.ds(q * hhalf, hhalf), pl.ds(j * half, half)],
+                )
+            )
+    for copy in [c_gn, c_geo, c_vec, c_low] + c_top:
         copy.wait()
 
 
@@ -441,15 +464,17 @@
         out_shape=(
             jax.ShapeDtypeStruct((n_count, half), BF16),
             jax.ShapeDtypeStruct((e_all, half), BF16),
-            jax.ShapeDtypeStruct((2, n_rows, half), BF16),
-            jax.ShapeDtypeStruct((2, e_rows, half), BF16),
+            jax.ShapeDtypeStruct((3 * width, hhalf), BF16),
+            jax.ShapeDtypeStruct((hhalf, width), BF16),
+            jax.ShapeDtypeStruct((2 * width, hid), BF16),
+            jax.ShapeDtypeStruct((hid, width), BF16),
             jax.ShapeDtypeStruct((8, width), F32),
         ),
         in_specs=[
             anywhere, anywhere, anywhere, anywhere, inside, inside, inside,
             anywhere, inside, anywhere, inside, anywhere, inside, anywhere, inside,
         ],
-        out_specs=(anywhere,) * 5,
+        out_specs=(anywhere,) * 7,
         scratch_shapes=[
             V((n_count, width), BF16),
             V((e_count, width), BF16),
@@ -498,7 +523,7 @@
             V((8, width), F32),
             V((steps + 1, 8, width), F32),
             V((1, hid), F32),
-            pltpu.SemaphoreType.DMA((16,)),
+            pltpu.SemaphoreType.DMA((32,)),
             pltpu.SemaphoreType.DMA((16 + 7 * steps,)),
             pltpu.SemaphoreType.DMA((16 + 7 * steps,)),
         ],
@@ -511,18 +536,13 @@
         edge_first, row(edge_bias), edge_second, row(edge_gain),
         node_first, row(node_bias), node_second, row(node_gain),
     )
-    g_nodes, g_edges, g_node, g_edge, vec = outs
-    side = lambda rows: jnp.concatenate(jnp.split(rows, 2, axis=0), axis=1)
-    g_node_first = jnp.concatenate([side(g_node[j, : 2 * width]) for j in range(2)], axis=0)
-    g_node_second = jnp.concatenate(
-        [side(g_node[j, 2 * width : 2 * width + 2 * hhalf]) for j in range(2)], axis=0
-    )
+    g_nodes, g_edges, g_first, g_second, g_node_first, g_node_second, vec = outs
     return (
         g_nodes[None],
         g_edges[None],
-        jnp.concatenate([g_edge[0, :width], g_edge[1, : 2 * width]], axis=0).astype(F32),
+        g_first.astype(F32),
         lax.dynamic_slice_in_dim(vec[0], part * hhalf, hhalf, 0),
-        side(g_edge[0, width : width + 2 * hhalf]).astype(F32),
+        g_second.astype(F32),
         vec[1],
         g_node_first.astype(F32),
         vec[2],

time: 85.9 us -> 85.9 us (level); the launches traced: 85.6 us -> 84.8 us
  local copies, waits for them, and re-layouts: 6.84 us -> 3.46 us
  other arithmetic: 4.82 us -> 6.11 us
  Pallas kernels: 73.3 us -> 74.5 us
    split x2 -> x0, local copies, waits for them, and re-layouts: 2.3 us -> none  [on_device(): side = lambda rows: jnp.concatenate(jnp.split(rows, 2, axis=0), axis=1)]
    convert_element_type x1, other arithmetic: 1.61 us -> 2.89 us  [on_device(): g_node_first.astype(F32)]
    pallas_call x1, Pallas kernels: 73.3 us -> 74.5 us  [on_device(): pl.pallas_call(functools.partial(kernel, (batches, patches, n_rows, e_row...]
    squeeze x1 -> x0, local copies, waits for them, and re-layouts: 1.08 us -> none  [on_device(): g_edge[1, :2 * width]]
where the time goes in v3:
time: 85.9 us; the launch traced here: 84.8 us
  Pallas kernels  74.5 us (87%)
  other arithmetic  6.11 us (7%)
  local copies, waits for them, and re-layouts  3.46 us (4%)
    pallas_call x1, Pallas kernels, on_device(): pl.pallas_call(functools.partial(kernel, (batches, patches, n_rows, e_row...  74.5 us
    convert_element_type x1, other arithmetic, on_device(): g_node_first.astype(F32)  2.89 us

profile of v3, /device:TPU:0, one launch (start us, length us, event | category | flops | bytes accessed | tf_op | source)
XLA Modules:
  0.0 84.8 jit_solution(490057881635784009)
XLA Ops:
  0.6 74.5 %shard_map.222 = (bf16[128,256]{1,0:T(8,128)(2,1)}, bf16[1024,256]{1,0:T(8,128)(2,1)}, bf16[1536,256]{1,0:T(8,128)(2,1)}, bf16[256,512]{1,0:T(8,128)(2,1)}, bf16...) custom-call(bf16[128,512]{1,0:T(8,128)(2,1)} %bitcast.20, bf16[1024,512]{1,0:T(8,128)(2,1)} %bitcast.17, ...), custom_call_target="tpu_custom_call" | custom-call | tf_op jit(solution)/shard_map/pallas_call | solution.py:462
  75.2 0.0 copy-start
  75.2 1.5 %fusion = (f32[1,512]{1,0:T(1,128)}, f32[1,512]{1,0:T(1,128)}, f32[1,512]{1,0:T(1,128)}, f32[1,512]{1,0:T(1,128)S(1)}) fusion(f32[8,512]{1,0:T(8,128)} %get-tuple-element.20), kind=kLoop, calls=%fused_computation.1 | loop fusion | bytes 16384 | tf_op jit(solution)/shard_map/slice | solution.py:550
  76.6 0.6 constant_dynamic-slice_fusion
  77.2 0.0 copy-start.1
  77.2 2.9 %convert_element_type.14 = f32[1024,512]{1,0:T(8,128)} convert(bf16[1024,512]{1,0:T(8,128)(2,1)} %get-tuple-element.22) | non-fusion elementwise | flops 524288 | bytes 3145728 | tf_op jit(solution)/shard_map/convert_element_type | solution.py:547
  80.1 0.0 copy-start.3
  80.1 0.0 copy-done
  80.1 0.0 copy-start.4
  80.1 0.0 copy-start.2
  80.1 1.3 %convert_element_type.12 = f32[1536,256]{1,0:T(8,128)} convert(bf16[1536,256]{1,0:T(8,128)(2,1)S(1)} %copy-done) | non-fusion elementwise | flops 393216 | bytes 2359296 | tf_op jit(solution)/shard_map/convert_element_type | solution.py:543
  81.4 0.0 copy-done.1
  81.4 1.1 %convert_element_type.15 = f32[512,512]{1,0:T(8,128)} convert(bf16[512,512]{1,0:T(8,128)(2,1)S(1)} %copy-done.1) | non-fusion elementwise | flops 262144 | bytes 1572864 | tf_op jit(solution)/shard_map/convert_element_type | solution.py:549
  82.5 0.0 copy-done.3
  82.5 0.9 %convert_element_type.13 = f32[256,512]{1,0:T(8,128)} convert(bf16[256,512]{1,0:T(8,128)(2,1)S(1)} %copy-done.3) | non-fusion elementwise | flops 131072 | bytes 786432 | tf_op jit(solution)/shard_map/convert_element_type | solution.py:545
  83.3 0.0 copy-done.4
  83.3 0.6 copy.27
  84.0 0.0 copy-done.2
  84.0 0.8 copy.28
Async XLA Ops:
  75.2 4.9 %copy-start = (bf16[1536,256]{1,0:T(8,128)(2,1)S(1)}, bf16[1536,256]{1,0:T(8,128)(2,1)}, u32[]{:S(2)}) copy-start(bf16[1536,256]{1,0:T(8,128)(2,1)} %get-tuple-element.19) | copy-start | bytes 2359300
  77.2 4.2 %copy-start.1 = (bf16[512,512]{1,0:T(8,128)(2,1)S(1)}, bf16[512,512]{1,0:T(8,128)(2,1)}, u32[]{:S(2)}) copy-start(bf16[512,512]{1,0:T(8,128)(2,1)} %get-tuple-element.23) | copy-start | bytes 1572868
  80.1 2.4 %copy-start.3 = (bf16[256,512]{1,0:T(8,128)(2,1)S(1)}, bf16[256,512]{1,0:T(8,128)(2,1)}, u32[]{:S(2)}) copy-start(bf16[256,512]{1,0:T(8,128)(2,1)} %get-tuple-element.21) | copy-start | bytes 786436
  80.1 3.2 %copy-start.4 = (bf16[128,256]{1,0:T(8,128)(2,1)S(1)}, bf16[128,256]{1,0:T(8,128)(2,1)}, u32[]{:S(2)}) copy-start(bf16[128,256]{1,0:T(8,128)(2,1)} %get-tuple-element.17) | copy-start | bytes 196612
  80.1 3.9 %copy-start.2 = (bf16[1024,256]{1,0:T(8,128)(2,1)S(1)}, bf16[1024,256]{1,0:T(8,128)(2,1)}, u32[]{:S(2)}) copy-start(bf16[1024,256]{1,0:T(8,128)(2,1)} %get-tuple-element.18) | copy-start | bytes 1572868
